TPU v7x, 1024 devices: a whole 8x8x8 slice. The times are simulated.
1024 devices in a mesh: dom: 64 (over x, z), sub: 16 (over y, core).
Axes of the slice: x: 8, y: 8, z: 8, core: 2. Of those that a mesh axis runs over, the one named last changes fastest.
Arguments:
- load_vector: float32 [2048, 128], P(('dom', 'sub')), may hold values from -38 to 38
- recycled: float32 [40, 2048, 128], P(None, ('dom', 'sub')), may hold values from -80 to 80
- images: float32 [40, 2048, 128], P(None, ('dom', 'sub')), may hold values from -6 to 6
- matrix_tiles: float32 [2048, 8, 128, 128], P(('dom', 'sub')), may hold values from -7 to 7
- tile_columns: int32 [2048, 8], P(('dom', 'sub')), may hold values from 0 to 5, as said below
- ghost_list: int32 [1024, 4], P(('dom', 'sub')), may hold values from 0 to 95, as said below
- live_counts: int32 [1024], P(('dom', 'sub')), may hold values from 1 to 2, as said below
Outputs:
- solution: float32 [2048, 128], P(('dom', 'sub'))
- residual: float32 [2048, 128], P(('dom', 'sub'))
Inputs may be any that keep to these rules, and one draw needn't show every extreme that they name: `live_counts`: each device's live block rows are its first slots; some device has all 2 live. `tile_columns`: tile 0 of a block row names the row's own slot. Other entries below 2 name a live slot of the same device; entries from 2 on name a ghost slot of that device. `ghost_list`: each entry names a live slot q of a device with sub index s and dom index differing from the owner's by o - 1 (o of 0, 1, 2), coded as o * (size of sub) * 2 + s * 2 + q; it never points outside the dom axis and never to the owner itself.
All inputs are finite; a program needn't handle non-finite values.
Results may differ from a plain program's by a relative error of at most 0.0003.
Values sent between devices are 32-bit elements; how exact they have to be, the bound alone decides.
A program may use at most 32 MiB of HBM per device.

v0:
```python
import functools

import jax
import jax.numpy as jnp
from jax import lax
from jax.sharding import Mesh
from jax.sharding import PartitionSpec as P

STEPS = 3
SUB = ("sub_0", "sub_1")
DOM = ("dom_0", "dom_1")
DOM_SUB = ("dom_0", "dom_1", "sub_0", "sub_1")


def padded(value, sides, width):
    for axis, dim in sides:
        count, length = (lax.axis_size(axis), value.shape[dim])
        up = [(i, (i + 1) % count) for i in range(count - 1)]
        down = [(j, i) for i, j in up]
        last = lax.slice_in_dim(value, length - width, length, axis=dim)
        first = lax.slice_in_dim(value, 0, width, axis=dim)
        before = lax.ppermute(last, axis, up)
        after = lax.ppermute(first, axis, down)
        value = jnp.concatenate([before, value, after], axis=dim)
    return value


def copy_for_each(value, axis):
    count = lax.axis_size(axis)
    return lax.all_to_all(
        jnp.broadcast_to(value[None], (count, *value.shape)), axis, 0, 0, tiled=True
    )


def joined_along(parts, dim):
    parts = jnp.moveaxis(parts, 0, dim)
    dims = parts.shape
    return parts.reshape(*dims[:dim], dims[dim] * dims[dim + 1], *dims[dim + 2 :])


def gather_directly(value, axis, dim):
    parts = copy_for_each(value, axis)
    return joined_along(parts, dim)


def by_axis(value, axes):
    return functools.reduce(lax.psum, axes, value)


def triangle_solve(factor, values, transpose):
    column = values if values.ndim == 2 else values[:, None]
    solved = lax.linalg.triangular_solve(
        factor, column, left_side=True, lower=True, transpose_a=transpose
    )
    return solved if values.ndim == 2 else solved[:, 0]


def multiply(vector, matrix_tiles, tile_columns, ghost_codes):
    slot_count = vector.shape[0]
    group_size = lax.axis_size(SUB) * slot_count
    dom_rows = padded(vector, ((DOM, 0),), slot_count)
    nearby = gather_directly(dom_rows, SUB, 0)
    offset = ghost_codes // group_size
    remainder = ghost_codes % group_size
    position = (
        remainder // slot_count * 3 * slot_count + offset * slot_count + remainder % slot_count
    )
    ghosts = jnp.take(nearby, position, axis=0)
    extended = jnp.concatenate([vector, ghosts], axis=0)
    picked = jnp.take(extended, tile_columns, axis=0)
    return jnp.einsum("stij,stj->si", matrix_tiles, picked, precision=lax.Precision.HIGHEST)


def local(load_vector, recycled, images, matrix_tiles, tile_columns, ghost_list, live_counts):
    highest = lax.Precision.HIGHEST
    slot_count, tile_width = load_vector.shape
    recycled_count = recycled.shape[0]
    live_mask = (jnp.arange(slot_count) < live_counts[0]).astype(jnp.float32)[:, None]
    ghost_codes = ghost_list[0]
    source = (load_vector * live_mask).reshape(-1)
    recycled_flat = (recycled * live_mask[None]).reshape(recycled_count, -1)
    images_flat = (images * live_mask[None]).reshape(recycled_count, -1)
    gram_matrix, projection, source_norm = (
        by_axis(jnp.dot(images_flat, images_flat.T, precision=highest), DOM_SUB),
        by_axis(jnp.dot(images_flat, source, precision=highest), DOM_SUB),
        by_axis(jnp.sum(source * source), DOM_SUB),
    )
    cholesky_low = jnp.linalg.cholesky(gram_matrix)
    reduced = triangle_solve(cholesky_low, projection, False)
    initial_norm = jnp.sqrt(source_norm - jnp.sum(reduced * reduced))
    images_hat = triangle_solve(cholesky_low, images_flat, False)
    recycled_hat = triangle_solve(cholesky_low, recycled_flat, False)
    start_point = jnp.dot(reduced, recycled_hat, precision=highest)
    start_residual = source - jnp.dot(reduced, images_hat, precision=highest)
    basis = [start_residual / initial_norm]
    hessenberg = jnp.zeros((STEPS + 1, STEPS), jnp.float32)
    coupling = jnp.zeros((recycled_count, STEPS), jnp.float32)
    for column in range(STEPS):
        image_now = multiply(
            basis[column].reshape(slot_count, tile_width), matrix_tiles, tile_columns, ghost_codes
        )
        image_now = (image_now * live_mask).reshape(-1)
        stacked = jnp.stack(basis)
        local_images = jnp.dot(images_hat, image_now, precision=highest)
        summed_images, against_basis, image_norm = (
            by_axis(local_images, DOM_SUB),
            by_axis(jnp.dot(stacked, image_now, precision=highest), DOM_SUB),
            by_axis(jnp.sum(image_now * image_now), DOM_SUB),
        )
        correction = jnp.dot(summed_images, images_hat, precision=highest)
        next_norm = jnp.sqrt(
            image_norm
            - jnp.sum(summed_images * summed_images)
            - jnp.sum(against_basis * against_basis)
        )
        remaining = image_now - correction - jnp.dot(against_basis, stacked, precision=highest)
        basis.append(remaining / next_norm)
        hessenberg = hessenberg.at[: column + 1, column].set(against_basis)
        hessenberg = hessenberg.at[column + 1, column].set(next_norm)
        coupling = coupling.at[:, column].set(summed_images)
    normal_matrix = jnp.dot(hessenberg.T, hessenberg, precision=highest)
    target = initial_norm * hessenberg[0]
    small_factor = jnp.linalg.cholesky(normal_matrix)
    least = triangle_solve(small_factor, triangle_solve(small_factor, target, False), True)
    every_basis = jnp.stack(basis)
    coupled = jnp.dot(coupling, least, precision=highest)
    recycled_term = jnp.dot(coupled, recycled_hat, precision=highest)
    solution = start_point + jnp.dot(least, every_basis[:STEPS], precision=highest) - recycled_term
    residual = start_residual - jnp.dot(
        jnp.dot(hessenberg, least, precision=highest), every_basis, precision=highest
    )
    return (solution.reshape(slot_count, tile_width), residual.reshape(slot_count, tile_width))


def solution(mesh):
    finer = Mesh(mesh.devices.reshape(8, 8, 8, 2), ("dom_0", "dom_1", "sub_0", "sub_1"))
    in_specs = (
        P(DOM_SUB, None),
        P(None, DOM_SUB, None),
        P(None, DOM_SUB, None),
        P(DOM_SUB, None, None, None),
        P(DOM_SUB, None),
        P(DOM_SUB, None),
        P(DOM_SUB),
    )
    out_specs = (P(DOM_SUB, None), P(DOM_SUB, None))
    return jax.shard_map(local, mesh=finer, in_specs=in_specs, out_specs=out_specs, check_vma=False)
```

profile of v0, /device:TPU:1, one launch (start us, length us, event | category | flops | bytes accessed | tf_op | source)
XLA Modules:
  0.0 375.6 jit_solution(8630245743654546472)
XLA Ops:
  1.4 0.7 copy-done.1
  2.1 0.7 multiply_reduce_fusion.4
  2.7 0.9 broadcast_multiply_fusion
  3.9 24.5 %all-reduce.13 = (f32[40,40]{0,1:T(8,128)S(1)}, f32[]{:T(128)}, f32[40]{0:T(128)S(1)}) all-reduce(f32[40,40]{0,1:T(8,128)S(1)} %convolution_bitcast_fusion, f32[]{:T(128)} %get-tuple-element.169, f32[40]{0:T(128)S(1)} %convolution_bitcast_fusion.5), channel_id=1, replica_groups=mesh['dom_0'=8,'dom_1'=8,'sub_0'=8,'sub_1'=2] {'dom_0'}, use_global_device_ids=true, to_apply=%region_0.0 | all-reduce | flops 1641 | bytes 13128 | tf_op jit(solution)/shard_map/psum | solution.py:47
  28.5 36.4 %all-reduce.9 = (f32[40,40]{0,1:T(8,128)S(1)}, f32[]{:T(128)}, f32[40]{0:T(128)S(1)}) all-reduce(f32[40,40]{0,1:T(8,128)S(1)} %get-tuple-element.146, f32[]{:T(128)} %get-tuple-element.147, f32[40]{0:T(128)S(1)} %get-tuple-element.148), channel_id=1, replica_groups=mesh['dom_0'=8,'dom_1'=8,'sub_0'=8,'sub_1'=2] {'dom_1'}, use_global_device_ids=true, to_apply=%region_1.0 | all-reduce | flops 1641 | bytes 13128 | tf_op jit(solution)/shard_map/psum | solution.py:47
  64.9 25.1 %all-reduce.5 = (f32[40,40]{0,1:T(8,128)S(1)}, f32[]{:T(128)}, f32[40]{0:T(128)S(1)}) all-reduce(f32[40,40]{0,1:T(8,128)S(1)} %get-tuple-element.134, f32[]{:T(128)} %get-tuple-element.135, f32[40]{0:T(128)S(1)} %get-tuple-element.136), channel_id=1, replica_groups=mesh['dom_0'=8,'dom_1'=8,'sub_0'=8,'sub_1'=2] {'sub_0'}, use_global_device_ids=true, to_apply=%region_2.0 | all-reduce | flops 1641 | bytes 13128 | tf_op jit(solution)/shard_map/psum | solution.py:47
  90.0 26.5 %all-reduce.17 = (f32[40,40]{0,1:T(8,128)S(1)}, f32[]{:T(128)}, f32[40]{0:T(128)S(1)}) all-reduce(f32[40,40]{0,1:T(8,128)S(1)} %get-tuple-element.122, f32[]{:T(128)} %get-tuple-element.123, f32[40]{0:T(128)S(1)} %get-tuple-element.124), channel_id=1, replica_groups=mesh['dom_0'=8,'dom_1'=8,'sub_0'=8,'sub_1'=2] {'sub_1'}, use_global_device_ids=true, to_apply=%region_3.0 | all-reduce | flops 1641 | bytes 13128 | tf_op jit(solution)/shard_map/psum | solution.py:47
  116.5 3.6 cholesky.29
  120.2 0.6 compare_reduce_fusion.4
  120.9 0.7 fusion.8
  121.5 3.1 custom-call.17
  124.8 0.7 fusion.48
  127.1 1.3 collective-permute-start.1
  128.4 4.0 %collective-permute-start = (f32[2,128]{1,0:T(2,128)S(1)}, f32[2,128]{1,0:T(2,128)S(1)}, u32[]{:S(2)}, u32[]{:S(2)}) collective-permute-start(f32[2,128]{1,0:T(2,128)S(1)} %bitcast.259), channel_id=1, source_target_pairs={{0,16},{16,32},{32,48},{48,64},{64,80},{80,96},{96,112},{112,128},... | collective-permute-start | bytes 3080 | tf_op jit(solution)/shard_map/ppermute | solution.py:22
  132.4 0.6 copy-done.4
  133.0 0.7 and_reduce_fusion
  134.2 0.6 compare_reduce_fusion.1
  134.9 0.6 broadcast_in_dim.26
  135.5 4.0 %all-to-all-start = ((f32[16,6,128]{2,1,0:T(8,128)}), f32[16,6,128]{2,1,0:T(8,128)S(1)}, u32[]{:S(2)}, u32[]{:S(2)}) async-start(f32[16,6,128]{2,1,0:T(8,128)} %broadcast_in_dim.26), calls=%async_computation | async-start | bytes 131072 | tf_op jit(solution)/shard_map/all_to_all | solution.py:30
  139.5 7.8 %all-to-all-done = f32[16,6,128]{2,1,0:T(8,128)S(1)} async-done(((f32[16,6,128]{2,1,0:T(8,128)}), f32[16,6,128]{2,1,0:T(8,128)S(1)}, u32[]{:S(2)}, u32[]{:S(2)}) %all-to-all-start) | async-done | bytes 49184 | tf_op jit(solution)/shard_map/all_to_all | solution.py:30
  148.6 1.0 fusion.62
  149.6 0.7 fusion.30
  150.3 0.6 multiply_reduce_fusion.3
  151.0 13.0 %all-reduce.12 = (f32[40]{0:T(128)S(1)}, f32[]{:T(128)}, f32[1]{0:T(128)}) all-reduce(f32[40]{0:T(128)S(1)} %convolution_bitcast_fusion.4, f32[]{:T(128)} %multiply_reduce_fusion.3, f32[1]{0:T(128)} %bitcast.27), channel_id=1, replica_groups=mesh['dom_0'=8,'dom_1'=8,'sub_0'=8,'sub_1'=2] {'dom_0'}, use_global_device_ids=true, to_apply=%region_25.29 | all-reduce | flops 42 | bytes 336 | tf_op jit(solution)/shard_map/psum | solution.py:47
  164.0 11.3 %all-reduce.8 = (f32[40]{0:T(128)S(1)}, f32[]{:T(128)}, f32[1]{0:T(128)}) all-reduce(f32[40]{0:T(128)S(1)} %get-tuple-element.143, f32[]{:T(128)} %get-tuple-element.144, f32[1]{0:T(128)} %get-tuple-element.145), channel_id=1, replica_groups=mesh['dom_0'=8,'dom_1'=8,'sub_0'=8,'sub_1'=2] {'dom_1'}, use_global_device_ids=true, to_apply=%region_26.30 | all-reduce | flops 42 | bytes 336 | tf_op jit(solution)/shard_map/psum | solution.py:47
  175.3 11.6 %all-reduce.4 = (f32[40]{0:T(128)S(1)}, f32[]{:T(128)}, f32[1]{0:T(128)}) all-reduce(f32[40]{0:T(128)S(1)} %get-tuple-element.131, f32[]{:T(128)} %get-tuple-element.132, f32[1]{0:T(128)} %get-tuple-element.133), channel_id=1, replica_groups=mesh['dom_0'=8,'dom_1'=8,'sub_0'=8,'sub_1'=2] {'sub_0'}, use_global_device_ids=true, to_apply=%region_27.31 | all-reduce | flops 42 | bytes 336 | tf_op jit(solution)/shard_map/psum | solution.py:47
  186.9 13.8 %all-reduce.16 = (f32[40]{0:T(128)S(1)}, f32[]{:T(128)}, f32[1]{0:T(128)}) all-reduce(f32[40]{0:T(128)S(1)} %get-tuple-element.119, f32[]{:T(128)} %get-tuple-element.120, f32[1]{0:T(128)} %get-tuple-element.121), channel_id=1, replica_groups=mesh['dom_0'=8,'dom_1'=8,'sub_0'=8,'sub_1'=2] {'sub_1'}, use_global_device_ids=true, to_apply=%region_28.32 | all-reduce | flops 42 | bytes 336 | tf_op jit(solution)/shard_map/psum | solution.py:47
  202.1 1.2 multiply_reduce_fusion.9
  204.6 0.7 fusion.32
  205.3 1.3 collective-permute-start.3
  206.6 4.3 %collective-permute-start.2 = (f32[2,128]{1,0:T(2,128)S(1)}, f32[2,128]{1,0:T(2,128)S(1)}, u32[]{:S(2)}, u32[]{:S(2)}) collective-permute-start(f32[2,128]{1,0:T(2,128)S(1)} %bitcast.270), channel_id=1, source_target_pairs={{0,16},{16,32},{32,48},{48,64},{64,80},{80,96},{96,112},{112,128},... | collective-permute-start | bytes 3080 | tf_op jit(solution)/shard_map/ppermute | solution.py:22
  211.4 0.7 compare_reduce_fusion
  212.2 0.6 broadcast_in_dim.27
  212.8 4.8 %all-to-all-start.1 = ((f32[16,6,128]{2,1,0:T(8,128)}), f32[16,6,128]{2,1,0:T(8,128)S(1)}, u32[]{:S(2)}, u32[]{:S(2)}) async-start(f32[16,6,128]{2,1,0:T(8,128)} %broadcast_in_dim.27), calls=%async_computation.1 | async-start | bytes 131072 | tf_op jit(solution)/shard_map/all_to_all | solution.py:30
  217.6 7.8 %all-to-all-done.1 = f32[16,6,128]{2,1,0:T(8,128)S(1)} async-done(((f32[16,6,128]{2,1,0:T(8,128)}), f32[16,6,128]{2,1,0:T(8,128)S(1)}, u32[]{:S(2)}, u32[]{:S(2)}) %all-to-all-start.1) | async-done | bytes 49184 | tf_op jit(solution)/shard_map/all_to_all | solution.py:30
  226.7 1.0 fusion.63
  227.7 0.7 multiply_reduce_fusion.2
  228.6 16.9 %all-reduce.11 = (f32[40]{0:T(128)S(1)}, f32[2]{0:T(128)S(1)}, f32[]{:T(128)}) all-reduce(f32[40]{0:T(128)S(1)} %convolution_bitcast_fusion.3, f32[2]{0:T(128)S(1)} %convolution_bitcast_fusion.10, f32[]{:T(128)} %get-tuple-element.163), channel_id=1, replica_groups=mesh['dom_0'=8,'dom_1'=8,'sub_0'=8,'sub_1'=2] {'dom_0'}, use_global_device_ids=true, to_apply=%region_40.44 | all-reduce | flops 43 | bytes 344 | tf_op jit(solution)/shard_map/psum | solution.py:47
  245.5 11.3 %all-reduce.7 = (f32[40]{0:T(128)S(1)}, f32[2]{0:T(128)S(1)}, f32[]{:T(128)}) all-reduce(f32[40]{0:T(128)S(1)} %get-tuple-element.140, f32[2]{0:T(128)S(1)} %get-tuple-element.141, f32[]{:T(128)} %get-tuple-element.142), channel_id=1, replica_groups=mesh['dom_0'=8,'dom_1'=8,'sub_0'=8,'sub_1'=2] {'dom_1'}, use_global_device_ids=true, to_apply=%region_41.45 | all-reduce | flops 43 | bytes 344 | tf_op jit(solution)/shard_map/psum | solution.py:47
  256.8 11.7 %all-reduce.3 = (f32[40]{0:T(128)S(1)}, f32[2]{0:T(128)S(1)}, f32[]{:T(128)}) all-reduce(f32[40]{0:T(128)S(1)} %get-tuple-element.128, f32[2]{0:T(128)S(1)} %get-tuple-element.129, f32[]{:T(128)} %get-tuple-element.130), channel_id=1, replica_groups=mesh['dom_0'=8,'dom_1'=8,'sub_0'=8,'sub_1'=2] {'sub_0'}, use_global_device_ids=true, to_apply=%region_42.46 | all-reduce | flops 43 | bytes 344 | tf_op jit(solution)/shard_map/psum | solution.py:47
  268.5 13.9 %all-reduce.15 = (f32[40]{0:T(128)S(1)}, f32[2]{0:T(128)S(1)}, f32[]{:T(128)}) all-reduce(f32[40]{0:T(128)S(1)} %get-tuple-element.116, f32[2]{0:T(128)S(1)} %get-tuple-element.117, f32[]{:T(128)} %get-tuple-element.118), channel_id=1, replica_groups=mesh['dom_0'=8,'dom_1'=8,'sub_0'=8,'sub_1'=2] {'sub_1'}, use_global_device_ids=true, to_apply=%region_43.47 | all-reduce | flops 43 | bytes 344 | tf_op jit(solution)/shard_map/psum | solution.py:47
  283.3 1.3 multiply_reduce_fusion.8
  286.5 1.3 collective-permute-start.5
  287.8 4.3 %collective-permute-start.4 = (f32[2,128]{1,0:T(2,128)S(1)}, f32[2,128]{1,0:T(2,128)S(1)}, u32[]{:S(2)}, u32[]{:S(2)}) collective-permute-start(f32[2,128]{1,0:T(2,128)S(1)} %bitcast.280), channel_id=1, source_target_pairs={{0,16},{16,32},{32,48},{48,64},{64,80},{80,96},{96,112},{112,128},... | collective-permute-start | bytes 3080 | tf_op jit(solution)/shard_map/ppermute | solution.py:22
  292.1 0.7 fusion.60
  292.8 0.7 compare_reduce_fusion.3
  293.4 0.6 scatter.30
  294.3 0.6 broadcast_in_dim.28
  294.9 4.8 %all-to-all-start.2 = ((f32[16,6,128]{2,1,0:T(8,128)}), f32[16,6,128]{2,1,0:T(8,128)S(1)}, u32[]{:S(2)}, u32[]{:S(2)}) async-start(f32[16,6,128]{2,1,0:T(8,128)} %broadcast_in_dim.28), calls=%async_computation.2 | async-start | bytes 131072 | tf_op jit(solution)/shard_map/all_to_all | solution.py:30
  299.7 1.9 broadcast_select_fusion.6
  301.6 1.3 scatter.34
  303.1 4.4 %all-to-all-done.2 = f32[16,6,128]{2,1,0:T(8,128)S(1)} async-done(((f32[16,6,128]{2,1,0:T(8,128)}), f32[16,6,128]{2,1,0:T(8,128)S(1)}, u32[]{:S(2)}, u32[]{:S(2)}) %all-to-all-start.2) | async-done | bytes 49184 | tf_op jit(solution)/shard_map/all_to_all | solution.py:30
  308.8 1.0 fusion.64
  309.8 0.7 multiply_reduce_fusion.1
  310.7 17.0 %all-reduce.10 = (f32[40]{0:T(128)S(1)}, f32[3]{0:T(128)S(1)}, f32[]{:T(128)}) all-reduce(f32[40]{0:T(128)S(1)} %convolution_bitcast_fusion.1, f32[3]{0:T(128)S(1)} %convolution_bitcast_fusion.2, f32[]{:T(128)} %get-tuple-element.161), channel_id=1, replica_groups=mesh['dom_0'=8,'dom_1'=8,'sub_0'=8,'sub_1'=2] {'dom_0'}, use_global_device_ids=true, to_apply=%region_56.60 | all-reduce | flops 44 | bytes 352 | tf_op jit(solution)/shard_map/psum | solution.py:47
  327.7 11.4 %all-reduce.6 = (f32[40]{0:T(128)S(1)}, f32[3]{0:T(128)S(1)}, f32[]{:T(128)}) all-reduce(f32[40]{0:T(128)S(1)} %get-tuple-element.137, f32[3]{0:T(128)S(1)} %get-tuple-element.138, f32[]{:T(128)} %get-tuple-element.139), channel_id=1, replica_groups=mesh['dom_0'=8,'dom_1'=8,'sub_0'=8,'sub_1'=2] {'dom_1'}, use_global_device_ids=true, to_apply=%region_57.61 | all-reduce | flops 44 | bytes 352 | tf_op jit(solution)/shard_map/psum | solution.py:47
  339.1 11.9 %all-reduce.2 = (f32[40]{0:T(128)S(1)}, f32[3]{0:T(128)S(1)}, f32[]{:T(128)}) all-reduce(f32[40]{0:T(128)S(1)} %get-tuple-element.125, f32[3]{0:T(128)S(1)} %get-tuple-element.126, f32[]{:T(128)} %get-tuple-element.127), channel_id=1, replica_groups=mesh['dom_0'=8,'dom_1'=8,'sub_0'=8,'sub_1'=2] {'sub_0'}, use_global_device_ids=true, to_apply=%region_58.62 | all-reduce | flops 44 | bytes 352 | tf_op jit(solution)/shard_map/psum | solution.py:47
  351.0 13.9 %all-reduce.14 = (f32[40]{0:T(128)S(1)}, f32[3]{0:T(128)S(1)}, f32[]{:T(128)}) all-reduce(f32[40]{0:T(128)S(1)} %get-tuple-element.113, f32[3]{0:T(128)S(1)} %get-tuple-element.114, f32[]{:T(128)} %get-tuple-element.115), channel_id=1, replica_groups=mesh['dom_0'=8,'dom_1'=8,'sub_0'=8,'sub_1'=2] {'sub_1'}, use_global_device_ids=true, to_apply=%region_59.63 | all-reduce | flops 44 | bytes 352 | tf_op jit(solution)/shard_map/psum | solution.py:47
  364.9 0.6 multiply_reduce_fusion.6
  365.6 0.6 multiply_reduce_fusion.5
  368.3 1.9 broadcast_select_fusion.5
  370.3 1.4 scatter.36
  372.5 0.6 compare_reduce_fusion.2
  373.1 0.6 fusion.22
  (89 shorter events, 10.7 us)
Async XLA Ops:
  0.6 148.0 %copy-start = (f32[2,8,128,128]{3,2,1,0:T(8,128)S(1)}, f32[2,8,128,128]{3,2,1,0:T(8,128)}, u32[]{:S(2)}) copy-start(f32[2,8,128,128]{3,2,1,0:T(8,128)} %param.34) | copy-start | bytes 3145732
  1.4 0.7 copy-start.1
  127.0 5.3 %copy-start.2 = (s32[2,8]{1,0:T(2,128)S(1)}, s32[2,8]{1,0:T(2,128)}, u32[]{:S(2)}) copy-start(s32[2,8]{1,0:T(2,128)} %param.35) | copy-start | bytes 196
  127.1 7.8 %collective-permute-start.1 = (f32[2,128]{1,0:T(2,128)S(1)}, f32[2,128]{1,0:T(2,128)S(1)}, u32[]{:S(2)}, u32[]{:S(2)}) collective-permute-start(f32[2,128]{1,0:T(2,128)S(1)} %bitcast.258), channel_id=1, source_target_pairs={{16,0},{32,16},{48,32},{64,48},{80,64},{96,80},{112,96},{128,112},... | collective-permute-start | bytes 3080 | tf_op jit(solution)/shard_map/ppermute | solution.py:23
  128.4 6.5 %collective-permute-start = (f32[2,128]{1,0:T(2,128)S(1)}, f32[2,128]{1,0:T(2,128)S(1)}, u32[]{:S(2)}, u32[]{:S(2)}) collective-permute-start(f32[2,128]{1,0:T(2,128)S(1)} %bitcast.259), channel_id=1, source_target_pairs={{0,16},{16,32},{32,48},{48,64},{64,80},{80,96},{96,112},{112,128},... | collective-permute-start | bytes 3080 | tf_op jit(solution)/shard_map/ppermute | solution.py:22
  132.4 0.7 copy-start.4
  133.0 0.7 copy-start.3
  135.5 11.8 %all-to-all-start = ((f32[16,6,128]{2,1,0:T(8,128)}), f32[16,6,128]{2,1,0:T(8,128)S(1)}, u32[]{:S(2)}, u32[]{:S(2)}) async-start(f32[16,6,128]{2,1,0:T(8,128)} %broadcast_in_dim.26), calls=%async_computation | async-start | bytes 131072 | tf_op jit(solution)/shard_map/all_to_all | solution.py:30
  205.3 6.9 %collective-permute-start.3 = (f32[2,128]{1,0:T(2,128)S(1)}, f32[2,128]{1,0:T(2,128)S(1)}, u32[]{:S(2)}, u32[]{:S(2)}) collective-permute-start(f32[2,128]{1,0:T(2,128)S(1)} %bitcast.269), channel_id=1, source_target_pairs={{16,0},{32,16},{48,32},{64,48},{80,64},{96,80},{112,96},{128,112},... | collective-permute-start | bytes 3080 | tf_op jit(solution)/shard_map/ppermute | solution.py:23
  206.6 5.6 %collective-permute-start.2 = (f32[2,128]{1,0:T(2,128)S(1)}, f32[2,128]{1,0:T(2,128)S(1)}, u32[]{:S(2)}, u32[]{:S(2)}) collective-permute-start(f32[2,128]{1,0:T(2,128)S(1)} %bitcast.270), channel_id=1, source_target_pairs={{0,16},{16,32},{32,48},{48,64},{64,80},{80,96},{96,112},{112,128},... | collective-permute-start | bytes 3080 | tf_op jit(solution)/shard_map/ppermute | solution.py:22
  212.8 12.6 %all-to-all-start.1 = ((f32[16,6,128]{2,1,0:T(8,128)}), f32[16,6,128]{2,1,0:T(8,128)S(1)}, u32[]{:S(2)}, u32[]{:S(2)}) async-start(f32[16,6,128]{2,1,0:T(8,128)} %broadcast_in_dim.27), calls=%async_computation.1 | async-start | bytes 131072 | tf_op jit(solution)/shard_map/all_to_all | solution.py:30
  286.5 7.7 %collective-permute-start.5 = (f32[2,128]{1,0:T(2,128)S(1)}, f32[2,128]{1,0:T(2,128)S(1)}, u32[]{:S(2)}, u32[]{:S(2)}) collective-permute-start(f32[2,128]{1,0:T(2,128)S(1)} %bitcast.279), channel_id=1, source_target_pairs={{16,0},{32,16},{48,32},{64,48},{80,64},{96,80},{112,96},{128,112},... | collective-permute-start | bytes 3080 | tf_op jit(solution)/shard_map/ppermute | solution.py:23
  287.8 6.4 %collective-permute-start.4 = (f32[2,128]{1,0:T(2,128)S(1)}, f32[2,128]{1,0:T(2,128)S(1)}, u32[]{:S(2)}, u32[]{:S(2)}) collective-permute-start(f32[2,128]{1,0:T(2,128)S(1)} %bitcast.280), channel_id=1, source_target_pairs={{0,16},{16,32},{32,48},{48,64},{64,80},{80,96},{96,112},{112,128},... | collective-permute-start | bytes 3080 | tf_op jit(solution)/shard_map/ppermute | solution.py:22
  294.9 12.6 %all-to-all-start.2 = ((f32[16,6,128]{2,1,0:T(8,128)}), f32[16,6,128]{2,1,0:T(8,128)S(1)}, u32[]{:S(2)}, u32[]{:S(2)}) async-start(f32[16,6,128]{2,1,0:T(8,128)} %broadcast_in_dim.28), calls=%async_computation.2 | async-start | bytes 131072 | tf_op jit(solution)/shard_map/all_to_all | solution.py:30
where the time goes:
time: 377 us; the launch traced here: 376 us
  blocking collectives  270 us (72%)
  starting transfers between devices  30.1 us (8%)
  other arithmetic  26.9 us (7%)
  waiting for transfers between devices  20 us (5%)
  local copies, waits for them, and re-layouts  11.9 us (3%)
  between operations  9.5 us (3%)
  matrix products  7.1 us (2%)
    psum x16, blocking collectives, by_axis(): return functools.reduce(lax.psum, axes, value)  270 us
    all_to_all x3, waiting for transfers between devices, copy_for_each(): lax.all_to_all(jnp.broadcast_to(value[None], (count, *value.shape)), axis...  20 us
    all_to_all x3, starting transfers between devices, copy_for_each(): lax.all_to_all(jnp.broadcast_to(value[None], (count, *value.shape)), axis...  13.7 us
    ppermute x3, starting transfers between devices, padded(): before = lax.ppermute(last, axis, up)  12.5 us
  transfers between devices with their start and end apart: 9, of which 3 were waited for; matrix products, arithmetic and copies ran while one was open for 2% of the time, Pallas kernels for 0%

commit v1 on v0

v1 whole, which is shorter than its diff:
```python
import functools

import jax
import jax.numpy as jnp
from jax import lax
from jax.experimental import pallas as pl
from jax.experimental.pallas import tpu as pltpu
from jax.sharding import PartitionSpec as P

MESH = pl.DeviceIdType.MESH
HIGHEST = lax.Precision.HIGHEST
K = 40
STEPS = 3
SLOTS = 2
TPR = 8
LANES = 128
ROWS = 48
NEW = 44
FOLD = 16


def iota(shape, dim):
    return lax.broadcasted_iota(jnp.int32, shape, dim)


def far_first(step, count):
    half = lax.div(step + 1, 2)
    return count // 2 + half * (1 - 2 * lax.rem(step, 2))


def landed(ref, pieces, sem):
    view = ref.at[pl.ds(0, pieces)]
    pltpu.make_async_copy(view, view, sem).wait()


def sweep(matrix, rows, lanes, count):
    for k in range(count):
        column = matrix[:, k : k + 1]
        pivot = 1.0 / matrix[k : k + 1, k : k + 1]
        row = jnp.where(lanes[:1] == k, 1.0, matrix[k : k + 1, :]) * pivot
        cleared = jnp.where(lanes == k, 0.0, matrix) - column * row
        matrix = jnp.where(rows == k, row, cleared)
    return matrix


def kernel(
    n_dom, n_z, n_sub,
    load_hbm, recycled_hbm, images_hbm, tiles_hbm, columns_ref, ghosts_ref, live_ref,
    solution_ref, residual_ref,
    source, recycled, images, tiles, stack, gram, halo,
    sub_wide, x_wide, z_wide, sub_thin, x_thin, z_thin,
    load_sem, wide_send, wide_recv, thin_send, thin_recv, halo_send, halo_recv,
):
    n_x = n_dom // n_z
    dom, sub = lax.axis_index("dom"), lax.axis_index("sub")
    x, z = lax.div(dom, n_z), lax.rem(dom, n_z)
    group = n_sub * SLOTS
    own = group + sub * SLOTS

    loads = [
        pltpu.make_async_copy(src, dst, load_sem.at[i])
        for i, (src, dst) in enumerate(
            [(images_hbm, images), (load_hbm, source), (tiles_hbm, tiles), (recycled_hbm, recycled)]
        )
    ]
    for load in loads:
        load.start()

    def sub_peer(step):
        return lax.rem(sub + far_first(step, n_sub), n_sub)

    def x_peer(step):
        return lax.rem(x + far_first(step, n_x), n_x) * n_z + z

    def z_peer(step):
        return x * n_z + lax.rem(z + far_first(step, n_z), n_z)

    def each(count, body):
        def wrapped(step, carry):
            body(step)
            return carry

        lax.fori_loop(0, count, wrapped, 0)

    barrier = pltpu.get_barrier_semaphore()

    def greet(device):
        pl.semaphore_signal(barrier, inc=1, device_id=device, device_id_type=MESH)

    before, after = lax.rem(dom + n_dom - 1, n_dom), lax.rem(dom + 1, n_dom)
    each(n_sub, lambda j: greet((before, sub_peer(j))))
    each(n_sub, lambda j: greet((after, sub_peer(j))))
    each(n_sub - 1, lambda j: greet((dom, sub_peer(j))))
    each(n_x - 1, lambda j: greet((x_peer(j), sub)))
    each(n_z - 1, lambda j: greet((z_peer(j), sub)))

    masks = [jnp.where(live_ref[0] > s, 1.0, 0.0) for s in range(SLOTS)]

    stack[...] = jnp.zeros_like(stack)
    loads[0].wait()
    loads[1].wait()
    for s in range(SLOTS):
        stack[s, 0:K, :] = images[:, s, :] * masks[s]
        stack[s, K : K + 1, :] = source[s : s + 1, :] * masks[s]
    packed = jnp.zeros((FOLD, LANES), jnp.float32)
    for part in range(3):
        rows_of = slice(14 * part, 14 * part + FOLD)
        block = sum(
            lax.dot_general(
                stack[s, rows_of, :], stack[s], (((1,), (1,)), ((), ())),
                precision=HIGHEST, preferred_element_type=jnp.float32,
            )
            for s in range(SLOTS)
        )
        packed = packed + (pltpu.roll(block, 41 * part, 1) if part else block)

    pl.semaphore_wait(barrier, 3 * n_sub - 1 + n_x - 1 + n_z - 1)

    def spread(buffer, place, count, peer, send, recv):
        mine = buffer.at[place]
        each(
            count - 1,
            lambda j: pltpu.make_async_remote_copy(
                src_ref=mine, dst_ref=mine, send_sem=send, recv_sem=recv,
                device_id=peer(j), device_id_type=MESH,
            ).start(),
        )
        landed(buffer, count - 1, recv)

    def summed(value, sub_buf, x_buf, z_buf, send, recv):
        sub_buf[sub] = value
        spread(sub_buf, sub, n_sub, lambda j: (dom, sub_peer(j)), send.at[0], recv.at[0])
        x_buf[x] = jnp.sum(sub_buf[...], axis=0)
        spread(x_buf, x, n_x, lambda j: (x_peer(j), sub), send.at[1], recv.at[1])
        z_buf[z] = jnp.sum(x_buf[...], axis=0)
        spread(z_buf, z, n_z, lambda j: (z_peer(j), sub), send.at[2], recv.at[2])
        return jnp.sum(z_buf[...], axis=0)

    rows, lanes = iota((ROWS, LANES), 0), iota((ROWS, LANES), 1)
    row_of = iota((ROWS, 1), 0)

    total = summed(packed, sub_wide, x_wide, z_wide, wide_send, wide_recv)
    for part in range(3):
        piece = pltpu.roll(total, LANES - 41 * part, 1) if part else total
        gram[14 * part : 14 * part + FOLD, :] = piece
    start = jnp.where((lanes <= K) & (rows <= K), gram[...], 0.0)
    swept = sweep(start, rows, lanes, K)
    unit = jnp.where(rows == lanes, 1.0, 0.0)
    inverse = jnp.where((rows < K) & (lanes < K), swept, jnp.where(rows < K, 0.0, unit))
    start_coef = jnp.where(row_of < K, swept[:, K : K + 1], 0.0)
    initial_norm = jnp.sqrt(swept[K : K + 1, K : K + 1])

    def combined(s, coef):
        return jnp.sum(stack[s, 0:ROWS, :] * coef, axis=0, keepdims=True)

    residuals = [stack[s, K : K + 1, :] - combined(s, start_coef) for s in range(SLOTS)]
    basis = [[r / initial_norm for r in residuals]]

    places = []
    for s in range(SLOTS):
        for t in range(TPR):
            column = columns_ref[s, t]
            ghost = ghosts_ref[0, jnp.clip(column - SLOTS, 0, 3)]
            places.append(jnp.where(column < SLOTS, own + column, ghost))

    def exchange(blocks, r):
        here = halo.at[r]
        for s in range(SLOTS):
            here[own + s] = blocks[s]
        mine = here.at[pl.ds(own, SLOTS)]

        def send(shift, device):
            there = here.at[pl.ds((1 - shift) * group + sub * SLOTS, SLOTS)]
            pltpu.make_async_remote_copy(
                src_ref=mine, dst_ref=there, send_sem=halo_send.at[r], recv_sem=halo_recv.at[r],
                device_id=device, device_id_type=MESH,
            ).start()

        def far(j):
            send(-1, (before, sub_peer(j)))
            send(1, (after, sub_peer(j)))

        each(n_sub, far)
        each(n_sub - 1, lambda j: send(0, (dom, sub_peer(j))))
        landed(here, 3 * group - SLOTS, halo_recv.at[r])

    def multiply(r):
        images_now = []
        for s in range(SLOTS):
            grid = jnp.zeros((LANES, LANES), jnp.float32)
            for t in range(TPR):
                grid = grid + tiles[s, t] * halo[r, places[s * TPR + t]]
            images_now.append(jnp.sum(grid.T, axis=0, keepdims=True) * masks[s])
        return images_now

    loads[2].wait()
    coefs, products, norms = [], [], []
    for step in range(STEPS):
        for s in range(SLOTS):
            stack[s, K + step : K + step + 1, :] = basis[step][s]
        exchange(basis[step], step)
        image = multiply(step)
        for s in range(SLOTS):
            stack[s, NEW : NEW + 1, :] = image[s]
        grid = sum(stack[s] * image[s] for s in range(SLOTS))
        dots = jnp.sum(grid.T, axis=0, keepdims=True)
        dots = summed(
            dots, sub_thin.at[step], x_thin.at[step], z_thin.at[step],
            thin_send.at[step], thin_recv.at[step],
        )
        coef = jnp.sum(inverse * dots, axis=1, keepdims=True)
        product = jnp.sum(unit * dots, axis=1, keepdims=True)
        square = jnp.sum(
            jnp.where(row_of < NEW, -coef * product, jnp.where(row_of == NEW, product, 0.0)),
            axis=0, keepdims=True,
        )
        coef = jnp.where(row_of < NEW, coef, 0.0)
        norm = jnp.sqrt(square)
        basis.append([(image[s] - combined(s, coef)) / norm for s in range(SLOTS)])
        coefs.append(jnp.where(row_of < K, coef, 0.0))
        products.append(product)
        norms.append(norm)

    hess = [[None] * STEPS for _ in range(STEPS + 1)]
    for j in range(STEPS):
        for i in range(j + 1):
            hess[i][j] = products[j][K + i : K + i + 1, :]
        hess[j + 1][j] = norms[j]
    normal = [
        [sum(hess[i][a] * hess[i][b] for i in range(min(a, b) + 2)) for b in range(STEPS)]
        for a in range(STEPS)
    ]
    right = [initial_norm * hess[0][j] for j in range(STEPS)]
    for k in range(STEPS):
        for i in range(k + 1, STEPS):
            ratio = normal[k][i] / normal[k][k]
            for j in range(i, STEPS):
                normal[i][j] = normal[i][j] - ratio * normal[k][j]
            right[i] = right[i] - ratio * right[k]
    least = [None] * STEPS
    for k in reversed(range(STEPS)):
        rest = right[k]
        for j in range(k + 1, STEPS):
            rest = rest - normal[k][j] * least[j]
        least[k] = rest / normal[k][k]
    weights = [
        sum(hess[i][j] * least[j] for j in range(max(i - 1, 0), STEPS)) for i in range(STEPS + 1)
    ]

    update = start_coef - sum(least[j] * coefs[j] for j in range(STEPS))
    loads[3].wait()
    for s in range(SLOTS):
        from_recycled = jnp.sum(recycled[:, s, :] * update[0:K], axis=0, keepdims=True) * masks[s]
        solution_ref[s : s + 1, :] = from_recycled + sum(
            least[j] * basis[j][s] for j in range(STEPS)
        )
        residual_ref[s : s + 1, :] = residuals[s] - sum(
            weights[i] * basis[i][s] for i in range(STEPS + 1)
        )

    landed(sub_wide, n_sub - 1, wide_send.at[0])
    landed(x_wide, n_x - 1, wide_send.at[1])
    landed(z_wide, n_z - 1, wide_send.at[2])
    for step in range(STEPS):
        landed(sub_thin.at[step], n_sub - 1, thin_send.at[step, 0])
        landed(x_thin.at[step], n_x - 1, thin_send.at[step, 1])
        landed(z_thin.at[step], n_z - 1, thin_send.at[step, 2])
        landed(halo.at[step], 3 * group - SLOTS, halo_send.at[step])


def build(mesh, n_z):
    n_dom, n_sub = mesh.shape["dom"], mesh.shape["sub"]
    n_x = n_dom // n_z
    f32 = jnp.float32

    def local(load_vector, recycled, images, matrix_tiles, tile_columns, ghost_list, live_counts):
        anywhere = pl.BlockSpec(memory_space=pl.ANY)
        scalars = pl.BlockSpec(memory_space=pltpu.SMEM)
        vectors = pl.BlockSpec(memory_space=pltpu.VMEM)
        shape = jax.ShapeDtypeStruct(load_vector.shape, f32)
        dma = pltpu.SemaphoreType.DMA
        return pl.pallas_call(
            functools.partial(kernel, n_dom, n_z, n_sub),
            out_shape=(shape, shape),
            in_specs=[anywhere] * 4 + [scalars] * 3,
            out_specs=(vectors, vectors),
            scratch_shapes=[
                pltpu.VMEM(load_vector.shape, f32),
                pltpu.VMEM(recycled.shape, f32),
                pltpu.VMEM(images.shape, f32),
                pltpu.VMEM(matrix_tiles.shape, f32),
                pltpu.VMEM((SLOTS, LANES, LANES), f32),
                pltpu.VMEM((ROWS, LANES), f32),
                pltpu.VMEM((STEPS, 3 * n_sub * SLOTS, 1, LANES), f32),
                pltpu.VMEM((n_sub, FOLD, LANES), f32),
                pltpu.VMEM((n_x, FOLD, LANES), f32),
                pltpu.VMEM((n_z, FOLD, LANES), f32),
                pltpu.VMEM((STEPS, n_sub, 1, LANES), f32),
                pltpu.VMEM((STEPS, n_x, 1, LANES), f32),
                pltpu.VMEM((STEPS, n_z, 1, LANES), f32),
                dma((4,)),
                dma((3,)), dma((3,)),
                dma((STEPS, 3)), dma((STEPS, 3)),
                dma((STEPS,)), dma((STEPS,)),
            ],
            compiler_params=pltpu.CompilerParams(collective_id=0, has_side_effects=True),
        )(load_vector, recycled, images, matrix_tiles, tile_columns, ghost_list, live_counts)

    both = ("dom", "sub")
    in_specs = (
        P(both, None),
        P(None, both, None),
        P(None, both, None),
        P(both, None, None, None),
        P(both, None),
        P(both, None),
        P(both),
    )
    out_specs = (P(both, None), P(both, None))
    return jax.shard_map(local, mesh=mesh, in_specs=in_specs, out_specs=out_specs, check_vma=False)


def solution(mesh):
    return build(mesh, 8)
```

time: 377 us -> 106 us (0.28)
  blocking collectives: 270 us -> 0 us
  Pallas kernels: 0 us -> 102 us
  starting transfers between devices: 30.1 us -> 0 us
  other arithmetic: 26.9 us -> 0 us
  waiting for transfers between devices: 20 us -> 0 us
  local copies, waits for them, and re-layouts: 11.9 us -> 1.85 us
  between operations: 9.5 us -> 1.3 us
  matrix products: 7.1 us -> 0 us
    psum x16 -> x0, blocking collectives: 270 us -> none  [by_axis(): return functools.reduce(lax.psum, axes, value)]
    pallas_call x0 -> x1, Pallas kernels: none -> 102 us  [local(): pl.pallas_call(functools.partial(kernel, n_dom, n_z, n_sub), out_shape=(s...]
    all_to_all x3 -> x0, waiting for transfers between devices: 20 us -> none  [copy_for_each(): lax.all_to_all(jnp.broadcast_to(value[None], (count, *value.shape)), axis...]
    another operation x17 -> x0, other arithmetic: 16.4 us -> none
    ppermute x6 -> x0, starting transfers between devices: 16.4 us -> none  [the longest x3 12.5 us: padded(): before = lax.ppermute(last, axis, up)]
    all_to_all x3 -> x0, starting transfers between devices: 13.7 us -> none  [copy_for_each(): lax.all_to_all(jnp.broadcast_to(value[None], (count, *value.shape)), axis...]
    reduce_sum x9 -> x0, other arithmetic: 6.97 us -> none  [the longest x3 3.14 us: local(): jnp.sum(summed_images * summed_images)]
    dot_general x23 -> x0, matrix products: 5.62 us -> none  [the longest x3 2.87 us: multiply(): jnp.einsum('stij,stj->si', matrix_tiles, picked, precision=lax.Precision....]
  transfers between devices with their start and end apart: 9 -> 0, of which waited for: 3 -> 0; matrix products, arithmetic and copies ran while one was open for 2% -> 0% of each run, Pallas kernels for 0% -> 0%
where the time goes in v1:
time: 106 us
  Pallas kernels  102 us (96%)
  local copies, waits for them, and re-layouts  1.85 us (2%)
  between operations  1.3 us (1%)
    pallas_call x1, Pallas kernels, local(): pl.pallas_call(functools.partial(kernel, n_dom, n_z, n_sub), out_shape=(s...  102 us

profile of v1, /device:TPU:1, one launch (start us, length us, event | category | flops | bytes accessed | tf_op | source)
XLA Modules:
  0.0 105.6 jit_solution(3690699523355432855)
XLA Ops:
  1.3 102.5 %shard_map.86 = (f32[2,128]{1,0:T(2,128)}, f32[2,128]{1,0:T(2,128)}) custom-call(f32[2,128]{1,0:T(2,128)} %load_hbm.1, f32[40,2,128]{2,1,0:T(2,128)} %recycled_hbm.1, f32[40,2,128]{2,1,0:T(2,128)} %images_hbm.1, f32[2,8,128,128]{3,2,1,0:T(8,128)} %tiles_hbm.1, s32[2,8]{1,0:T(2,128)} %columns_ref.1, s32[1,4]{1,0:T(1,128)} %ghosts_ref.1, s32[1]{0:T(128)S(6)} %copy.11.live_ref), custom_call_target="tpu_custom_call" | custom-call | tf_op jit(solution)/shard_map/pallas_call | solution.py:282
  103.8 0.0 copy-start.1
  103.8 0.7 copy-done.1
  104.4 0.0 copy-start
  104.4 0.6 copy.12
  105.0 0.1 copy-done
  105.1 0.6 copy.13
Async XLA Ops:
  103.8 0.7 copy-start.1
  104.4 0.6 copy-start

commit v2 on v1

--- a/solution.py
+++ b/solution.py
@@ -13,6 +13,9 @@
 STEPS = 3
 SLOTS = 2
 TPR = 8
+GHOSTS = 4
+BLOCKS = SLOTS + GHOSTS
+CORES = 2
 LANES = 128
 ROWS = 48
 NEW = 44
@@ -47,13 +50,17 @@
     n_dom, n_z, n_sub,
     load_hbm, recycled_hbm, images_hbm, tiles_hbm, columns_ref, ghosts_ref, live_ref,
     solution_ref, residual_ref,
-    source, recycled, images, tiles, stack, gram, halo,
-    sub_wide, x_wide, z_wide, sub_thin, x_thin, z_thin,
-    load_sem, wide_send, wide_recv, thin_send, thin_recv, halo_send, halo_recv,
+    source, recycled, images, tiles, stack, ghost_stack, gram, vectors, *more,
 ):
+    halos, more = more[: STEPS - 1], more[STEPS - 1 :]
+    line, asks, ask, asked, answers, answered, *more = more
+    sub_wide, x_wide, z_wide, sub_thin, x_thin, z_thin, load_sem, *more = more
+    wide_send, wide_recv, thin_send, thin_recv, halo_send, halo_recv, near_send, near_recv = more
     n_x = n_dom // n_z
+    n_y = n_sub // CORES
     dom, sub = lax.axis_index("dom"), lax.axis_index("sub")
     x, z = lax.div(dom, n_z), lax.rem(dom, n_z)
+    y, core = lax.div(sub, CORES), lax.rem(sub, CORES)
     group = n_sub * SLOTS
     own = group + sub * SLOTS
 
@@ -69,6 +76,9 @@
     def sub_peer(step):
         return lax.rem(sub + far_first(step, n_sub), n_sub)
 
+    def y_peer(step):
+        return lax.rem(y + far_first(step, n_y), n_y) * CORES + core
+
     def x_peer(step):
         return lax.rem(x + far_first(step, n_x), n_x) * n_z + z
 
@@ -95,13 +105,22 @@
     each(n_z - 1, lambda j: greet((z_peer(j), sub)))
 
     masks = [jnp.where(live_ref[0] > s, 1.0, 0.0) for s in range(SLOTS)]
-
+    rows, lanes = iota((ROWS, LANES), 0), iota((ROWS, LANES), 1)
+    row_of = iota((ROWS, 1), 0)
+
+    ghost_codes = [ghosts_ref[0, g] for g in range(GHOSTS)]
+    request = jnp.zeros((1, LANES), jnp.int32)
+    for g in range(GHOSTS):
+        request = jnp.where(lanes[:1] == g, ghost_codes[g], request)
+    ask[0] = request
+    asks[CORES + core] = request
     stack[...] = jnp.zeros_like(stack)
     loads[0].wait()
     loads[1].wait()
     for s in range(SLOTS):
         stack[s, 0:K, :] = images[:, s, :] * masks[s]
         stack[s, K : K + 1, :] = source[s : s + 1, :] * masks[s]
+        line[y, s] = stack[s, 0:ROWS, :]
     packed = jnp.zeros((FOLD, LANES), jnp.float32)
     for part in range(3):
         rows_of = slice(14 * part, 14 * part + FOLD)
@@ -116,30 +135,61 @@
 
     pl.semaphore_wait(barrier, 3 * n_sub - 1 + n_x - 1 + n_z - 1)
 
+    def push(src, dst, send, recv, device):
+        pltpu.make_async_remote_copy(
+            src_ref=src, dst_ref=dst, send_sem=send, recv_sem=recv,
+            device_id=device, device_id_type=MESH,
+        ).start()
+
     def spread(buffer, place, count, peer, send, recv):
         mine = buffer.at[place]
-        each(
-            count - 1,
-            lambda j: pltpu.make_async_remote_copy(
-                src_ref=mine, dst_ref=mine, send_sem=send, recv_sem=recv,
-                device_id=peer(j), device_id_type=MESH,
-            ).start(),
-        )
-        landed(buffer, count - 1, recv)
-
-    def summed(value, sub_buf, x_buf, z_buf, send, recv):
-        sub_buf[sub] = value
-        spread(sub_buf, sub, n_sub, lambda j: (dom, sub_peer(j)), send.at[0], recv.at[0])
-        x_buf[x] = jnp.sum(sub_buf[...], axis=0)
-        spread(x_buf, x, n_x, lambda j: (x_peer(j), sub), send.at[1], recv.at[1])
-        z_buf[z] = jnp.sum(x_buf[...], axis=0)
-        spread(z_buf, z, n_z, lambda j: (z_peer(j), sub), send.at[2], recv.at[2])
-        return jnp.sum(z_buf[...], axis=0)
-
-    rows, lanes = iota((ROWS, LANES), 0), iota((ROWS, LANES), 1)
-    row_of = iota((ROWS, 1), 0)
-
-    total = summed(packed, sub_wide, x_wide, z_wide, wide_send, wide_recv)
+        each(count - 1, lambda j: push(mine, mine, send, recv, peer(j)))
+
+    near = [
+        (shift, other)
+        for shift in (-1, 1, 0)
+        for other in ((0, 1) if shift else (1,))
+    ]
+    dom_at = {-1: before, 0: dom, 1: after}
+
+    def core_at(other):
+        return 1 - core if other else core
+
+    sub_wide[sub] = packed
+    spread(sub_wide, sub, n_sub, lambda j: (dom, sub_peer(j)), wide_send.at[0], wide_recv.at[0])
+    for shift, other in near:
+        device = (dom_at[shift], y * CORES + core_at(other))
+        place = (1 - shift) * CORES + core
+        push(ask.at[0], asks.at[place], near_send.at[0], near_recv.at[0], device)
+    spread(line, y, n_y, lambda j: (dom, y_peer(j)), near_send.at[1], near_recv.at[1])
+    landed(sub_wide, n_sub - 1, wide_recv.at[0])
+    z_wide[z] = jnp.sum(sub_wide[...], axis=0)
+    spread(z_wide, z, n_z, lambda j: (z_peer(j), sub), wide_send.at[1], wide_recv.at[1])
+    landed(asks, len(near), near_recv.at[0])
+    listed = pltpu.make_async_copy(asks, asked, load_sem.at[4])
+    listed.start()
+    listed.wait()
+    landed(z_wide, n_z - 1, wide_recv.at[1])
+    x_wide[x] = jnp.sum(z_wide[...], axis=0)
+    spread(x_wide, x, n_x, lambda j: (x_peer(j), sub), wide_send.at[2], wide_recv.at[2])
+    landed(line, n_y - 1, near_recv.at[1])
+
+    def place_of(code):
+        rest = lax.rem(code, group)
+        return lax.div(rest, CORES * SLOTS), lax.rem(rest, SLOTS)
+
+    for i, (shift, other) in enumerate(near):
+        asker = (1 + shift) * CORES + core_at(other)
+        for g in range(GHOSTS):
+            answers[i, g] = line[place_of(asked[asker, 0, g])]
+        device = (dom_at[shift], y * CORES + core_at(other))
+        place = (1 - shift) * CORES + core
+        push(answers.at[i], answered.at[place], near_send.at[2], near_recv.at[2], device)
+    for g in range(GHOSTS):
+        answered[CORES + core, g] = line[place_of(ghost_codes[g])]
+    landed(x_wide, n_x - 1, wide_recv.at[2])
+    total = jnp.sum(x_wide[...], axis=0)
+
     for part in range(3):
         piece = pltpu.roll(total, LANES - 41 * part, 1) if part else total
         gram[14 * part : 14 * part + FOLD, :] = piece
@@ -150,64 +200,79 @@
     start_coef = jnp.where(row_of < K, swept[:, K : K + 1], 0.0)
     initial_norm = jnp.sqrt(swept[K : K + 1, K : K + 1])
 
-    def combined(s, coef):
-        return jnp.sum(stack[s, 0:ROWS, :] * coef, axis=0, keepdims=True)
-
-    residuals = [stack[s, K : K + 1, :] - combined(s, start_coef) for s in range(SLOTS)]
+    landed(answered, len(near), near_recv.at[2])
+    for g in range(GHOSTS):
+        code = ghost_codes[g]
+        held = lax.div(code, group) * CORES + lax.rem(lax.div(code, SLOTS), CORES)
+        ghost_stack[g] = answered[held, g]
+
+    def block(e):
+        return stack[e, 0:ROWS, :] if e < SLOTS else ghost_stack[e - SLOTS]
+
+    def combined(e, coef):
+        return jnp.sum(block(e) * coef, axis=0, keepdims=True)
+
+    def put(vector, step):
+        for e, part in enumerate(vector):
+            row = slice(K + step, K + step + 1)
+            if e < SLOTS:
+                stack[e, row, :] = part
+            else:
+                ghost_stack[e - SLOTS, row, :] = part
+            vectors[step, e] = part
+
+    residuals = [block(e)[K : K + 1, :] - combined(e, start_coef) for e in range(BLOCKS)]
     basis = [[r / initial_norm for r in residuals]]
 
-    places = []
-    for s in range(SLOTS):
-        for t in range(TPR):
-            column = columns_ref[s, t]
-            ghost = ghosts_ref[0, jnp.clip(column - SLOTS, 0, 3)]
-            places.append(jnp.where(column < SLOTS, own + column, ghost))
-
-    def exchange(blocks, r):
-        here = halo.at[r]
+    def send_halo(blocks, r):
+        here = halos[r]
         for s in range(SLOTS):
             here[own + s] = blocks[s]
         mine = here.at[pl.ds(own, SLOTS)]
 
-        def send(shift, device):
+        def to(shift, device):
             there = here.at[pl.ds((1 - shift) * group + sub * SLOTS, SLOTS)]
-            pltpu.make_async_remote_copy(
-                src_ref=mine, dst_ref=there, send_sem=halo_send.at[r], recv_sem=halo_recv.at[r],
-                device_id=device, device_id_type=MESH,
-            ).start()
+            push(mine, there, halo_send.at[r], halo_recv.at[r], device)
 
         def far(j):
-            send(-1, (before, sub_peer(j)))
-            send(1, (after, sub_peer(j)))
+            to(-1, (before, sub_peer(j)))
+            to(1, (after, sub_peer(j)))
 
         each(n_sub, far)
-        each(n_sub - 1, lambda j: send(0, (dom, sub_peer(j))))
-        landed(here, 3 * group - SLOTS, halo_recv.at[r])
-
-    def multiply(r):
-        images_now = []
+        each(n_sub - 1, lambda j: to(0, (dom, sub_peer(j))))
+
+    def multiply(step):
+        image = []
         for s in range(SLOTS):
             grid = jnp.zeros((LANES, LANES), jnp.float32)
             for t in range(TPR):
-                grid = grid + tiles[s, t] * halo[r, places[s * TPR + t]]
-            images_now.append(jnp.sum(grid.T, axis=0, keepdims=True) * masks[s])
-        return images_now
+                grid = grid + tiles[s, t] * vectors[step, columns_ref[s, t]]
+            image.append(jnp.sum(grid.T, axis=0, keepdims=True) * masks[s])
+        return image
 
     loads[2].wait()
     coefs, products, norms = [], [], []
     for step in range(STEPS):
-        for s in range(SLOTS):
-            stack[s, K + step : K + step + 1, :] = basis[step][s]
-        exchange(basis[step], step)
+        last = step == STEPS - 1
+        put(basis[step], step)
         image = multiply(step)
         for s in range(SLOTS):
             stack[s, NEW : NEW + 1, :] = image[s]
         grid = sum(stack[s] * image[s] for s in range(SLOTS))
-        dots = jnp.sum(grid.T, axis=0, keepdims=True)
-        dots = summed(
-            dots, sub_thin.at[step], x_thin.at[step], z_thin.at[step],
-            thin_send.at[step], thin_recv.at[step],
-        )
+        across, down, along = sub_thin.at[step], z_thin.at[step], x_thin.at[step]
+        send, recv = thin_send.at[step], thin_recv.at[step]
+        across[sub] = jnp.sum(grid.T, axis=0, keepdims=True)
+        spread(across, sub, n_sub, lambda j: (dom, sub_peer(j)), send.at[0], recv.at[0])
+        if not last:
+            send_halo(image, step)
+        landed(across, n_sub - 1, recv.at[0])
+        down[z] = jnp.sum(across[...], axis=0)
+        spread(down, z, n_z, lambda j: (z_peer(j), sub), send.at[1], recv.at[1])
+        landed(down, n_z - 1, recv.at[1])
+        along[x] = jnp.sum(down[...], axis=0)
+        spread(along, x, n_x, lambda j: (x_peer(j), sub), send.at[2], recv.at[2])
+        landed(along, n_x - 1, recv.at[2])
+        dots = jnp.sum(along[...], axis=0)
         coef = jnp.sum(inverse * dots, axis=1, keepdims=True)
         product = jnp.sum(unit * dots, axis=1, keepdims=True)
         square = jnp.sum(
@@ -216,7 +281,10 @@
         )
         coef = jnp.where(row_of < NEW, coef, 0.0)
         norm = jnp.sqrt(square)
-        basis.append([(image[s] - combined(s, coef)) / norm for s in range(SLOTS)])
+        if not last:
+            landed(halos[step], 3 * group - SLOTS, halo_recv.at[step])
+            image = image + [halos[step][ghost_codes[g]] for g in range(GHOSTS)]
+        basis.append([(part - combined(e, coef)) / norm for e, part in enumerate(image)])
         coefs.append(jnp.where(row_of < K, coef, 0.0))
         products.append(product)
         norms.append(norm)
@@ -259,18 +327,22 @@
         )
 
     landed(sub_wide, n_sub - 1, wide_send.at[0])
-    landed(x_wide, n_x - 1, wide_send.at[1])
-    landed(z_wide, n_z - 1, wide_send.at[2])
+    landed(z_wide, n_z - 1, wide_send.at[1])
+    landed(x_wide, n_x - 1, wide_send.at[2])
+    landed(asks, len(near), near_send.at[0])
+    landed(line, n_y - 1, near_send.at[1])
+    landed(answers, len(near), near_send.at[2])
     for step in range(STEPS):
         landed(sub_thin.at[step], n_sub - 1, thin_send.at[step, 0])
-        landed(x_thin.at[step], n_x - 1, thin_send.at[step, 1])
-        landed(z_thin.at[step], n_z - 1, thin_send.at[step, 2])
-        landed(halo.at[step], 3 * group - SLOTS, halo_send.at[step])
+        landed(z_thin.at[step], n_z - 1, thin_send.at[step, 1])
+        landed(x_thin.at[step], n_x - 1, thin_send.at[step, 2])
+        if step < STEPS - 1:
+            landed(halos[step], 3 * group - SLOTS, halo_send.at[step])
 
 
 def build(mesh, n_z):
     n_dom, n_sub = mesh.shape["dom"], mesh.shape["sub"]
-    n_x = n_dom // n_z
+    n_x, n_y = n_dom // n_z, n_sub // CORES
     f32 = jnp.float32
 
     def local(load_vector, recycled, images, matrix_tiles, tile_columns, ghost_list, live_counts):
@@ -279,6 +351,7 @@
         vectors = pl.BlockSpec(memory_space=pltpu.VMEM)
         shape = jax.ShapeDtypeStruct(load_vector.shape, f32)
         dma = pltpu.SemaphoreType.DMA
+        asks = (3 * CORES, 1, LANES)
         return pl.pallas_call(
             functools.partial(kernel, n_dom, n_z, n_sub),
             out_shape=(shape, shape),
@@ -290,18 +363,27 @@
                 pltpu.VMEM(images.shape, f32),
                 pltpu.VMEM(matrix_tiles.shape, f32),
                 pltpu.VMEM((SLOTS, LANES, LANES), f32),
+                pltpu.VMEM((GHOSTS, ROWS, LANES), f32),
                 pltpu.VMEM((ROWS, LANES), f32),
-                pltpu.VMEM((STEPS, 3 * n_sub * SLOTS, 1, LANES), f32),
+                pltpu.VMEM((STEPS, BLOCKS, 1, LANES), f32),
+                *[pltpu.VMEM((3 * n_sub * SLOTS, 1, LANES), f32)] * (STEPS - 1),
+                pltpu.VMEM((n_y, SLOTS, ROWS, LANES), f32),
+                pltpu.VMEM(asks, jnp.int32),
+                pltpu.VMEM((1, 1, LANES), jnp.int32),
+                pltpu.SMEM(asks, jnp.int32),
+                pltpu.VMEM((3 * CORES - 1, GHOSTS, ROWS, LANES), f32),
+                pltpu.VMEM((3 * CORES, GHOSTS, ROWS, LANES), f32),
                 pltpu.VMEM((n_sub, FOLD, LANES), f32),
                 pltpu.VMEM((n_x, FOLD, LANES), f32),
                 pltpu.VMEM((n_z, FOLD, LANES), f32),
                 pltpu.VMEM((STEPS, n_sub, 1, LANES), f32),
                 pltpu.VMEM((STEPS, n_x, 1, LANES), f32),
                 pltpu.VMEM((STEPS, n_z, 1, LANES), f32),
-                dma((4,)),
+                dma((5,)),
                 dma((3,)), dma((3,)),
                 dma((STEPS, 3)), dma((STEPS, 3)),
-                dma((STEPS,)), dma((STEPS,)),
+                dma((STEPS - 1,)), dma((STEPS - 1,)),
+                dma((3,)), dma((3,)),
             ],
             compiler_params=pltpu.CompilerParams(collective_id=0, has_side_effects=True),
         )(load_vector, recycled, images, matrix_tiles, tile_columns, ghost_list, live_counts)

time: 106 us -> 90.3 us (0.85)
  Pallas kernels: 102 us -> 86.6 us
    pallas_call x1, Pallas kernels: 102 us -> 86.6 us  [local(): pl.pallas_call(functools.partial(kernel, n_dom, n_z, n_sub), out_shape=(s...]
where the time goes in v2:
time: 90.3 us; the launch traced here: 89.7 us
  Pallas kernels  86.6 us (96%)
  local copies, waits for them, and re-layouts  1.85 us (2%)
  between operations  1.3 us (1%)
    pallas_call x1, Pallas kernels, local(): pl.pallas_call(functools.partial(kernel, n_dom, n_z, n_sub), out_shape=(s...  86.6 us
    unnamed x6, local copies, waits for them, and re-layouts  1.85 us

profile of v2, /device:TPU:1, one launch (start us, length us, event | category | flops | bytes accessed | tf_op | source)
XLA Modules:
  0.0 89.7 jit_solution(17244110618688965185)
XLA Ops:
  1.3 86.6 %shard_map.86 = (f32[2,128]{1,0:T(2,128)}, f32[2,128]{1,0:T(2,128)}) custom-call(f32[2,128]{1,0:T(2,128)} %load_hbm.1, f32[40,2,128]{2,1,0:T(2,128)} %recycled_hbm.1, f32[40,2,128]{2,1,0:T(2,128)} %images_hbm.1, f32[2,8,128,128]{3,2,1,0:T(8,128)} %tiles_hbm.1, s32[2,8]{1,0:T(2,128)} %columns_ref.1, s32[1,4]{1,0:T(1,128)} %ghosts_ref.1, s32[1]{0:T(128)S(6)} %copy.11.live_ref), custom_call_target="tpu_custom_call" | custom-call | tf_op jit(solution)/shard_map/pallas_call | solution.py:355
  87.9 0.0 copy-start.1
  87.9 0.7 copy-done.1
  88.5 0.0 copy-start
  88.5 0.6 copy.12
  89.1 0.1 copy-done
  89.2 0.6 copy.13
Async XLA Ops:
  87.9 0.7 copy-start.1
  88.5 0.6 copy-start

commit v3 on v2

--- a/solution.py
+++ b/solution.py
@@ -16,6 +16,7 @@
 GHOSTS = 4
 BLOCKS = SLOTS + GHOSTS
 CORES = 2
+PIVOTS = 4
 LANES = 128
 ROWS = 48
 NEW = 44
@@ -37,25 +38,31 @@
 
 
 def sweep(matrix, rows, lanes, count):
-    for k in range(count):
-        column = matrix[:, k : k + 1]
-        pivot = 1.0 / matrix[k : k + 1, k : k + 1]
-        row = jnp.where(lanes[:1] == k, 1.0, matrix[k : k + 1, :]) * pivot
-        cleared = jnp.where(lanes == k, 0.0, matrix) - column * row
-        matrix = jnp.where(rows == k, row, cleared)
+    for first in range(0, count, PIVOTS):
+        steps = range(first, first + PIVOTS)
+        columns = [jnp.broadcast_to(matrix[:, k : k + 1], matrix.shape) for k in steps]
+        for i, k in enumerate(steps):
+            column = columns[i]
+            pivot = 1.0 / column[k : k + 1, :]
+            row = jnp.where(lanes[:1] == k, 1.0, matrix[k : k + 1, :]) * pivot
+            cleared = jnp.where(lanes == k, 0.0, matrix) - column * row
+            matrix = jnp.where(rows == k, row, cleared)
+            for j in range(i + 1, PIVOTS):
+                scale = columns[j][k : k + 1, :] * pivot
+                columns[j] = jnp.where(rows == k, scale, columns[j] - column * scale)
     return matrix
 
 
 def kernel(
     n_dom, n_z, n_sub,
     load_hbm, recycled_hbm, images_hbm, tiles_hbm, columns_ref, ghosts_ref, live_ref,
-    solution_ref, residual_ref,
+    parts_ref,
     source, recycled, images, tiles, stack, ghost_stack, gram, vectors, *more,
 ):
     halos, more = more[: STEPS - 1], more[STEPS - 1 :]
     line, asks, ask, asked, answers, answered, *more = more
     sub_wide, x_wide, z_wide, sub_thin, x_thin, z_thin, load_sem, *more = more
-    wide_send, wide_recv, thin_send, thin_recv, halo_send, halo_recv, near_send, near_recv = more
+    wide_send, wide_recv, thin_send, thin_recv, halo_send, halo_recv, near_send, near_recv, hop_recv = more
     n_x = n_dom // n_z
     n_y = n_sub // CORES
     dom, sub = lax.axis_index("dom"), lax.axis_index("sub")
@@ -75,9 +82,6 @@
 
     def sub_peer(step):
         return lax.rem(sub + far_first(step, n_sub), n_sub)
-
-    def y_peer(step):
-        return lax.rem(y + far_first(step, n_y), n_y) * CORES + core
 
     def x_peer(step):
         return lax.rem(x + far_first(step, n_x), n_x) * n_z + z
@@ -145,6 +149,10 @@
         mine = buffer.at[place]
         each(count - 1, lambda j: push(mine, mine, send, recv, peer(j)))
 
+    def along_y(piece, hops, send, recv):
+        device = (dom, lax.rem(y + hops + n_y, n_y) * CORES + core)
+        push(piece, piece, send, recv, device)
+
     near = [
         (shift, other)
         for shift in (-1, 1, 0)
@@ -161,10 +169,16 @@
         device = (dom_at[shift], y * CORES + core_at(other))
         place = (1 - shift) * CORES + core
         push(ask.at[0], asks.at[place], near_send.at[0], near_recv.at[0], device)
-    spread(line, y, n_y, lambda j: (dom, y_peer(j)), near_send.at[1], near_recv.at[1])
+    for i, hops in enumerate((2, -2, 1, -1)):
+        along_y(line.at[y], hops, near_send.at[1], hop_recv.at[i])
     landed(sub_wide, n_sub - 1, wide_recv.at[0])
     z_wide[z] = jnp.sum(sub_wide[...], axis=0)
     spread(z_wide, z, n_z, lambda j: (z_peer(j), sub), wide_send.at[1], wide_recv.at[1])
+    for i, sign in enumerate((1, -1)):
+        landed(line, 1, hop_recv.at[i])
+        held = line.at[lax.rem(y - 2 * sign + n_y, n_y)]
+        along_y(held, sign, near_send.at[1], hop_recv.at[4 + i])
+        along_y(held.at[pl.ds(i, 1)], 2 * sign, near_send.at[1], hop_recv.at[6 + i])
     landed(asks, len(near), near_recv.at[0])
     listed = pltpu.make_async_copy(asks, asked, load_sem.at[4])
     listed.start()
@@ -172,7 +186,10 @@
     landed(z_wide, n_z - 1, wide_recv.at[1])
     x_wide[x] = jnp.sum(z_wide[...], axis=0)
     spread(x_wide, x, n_x, lambda j: (x_peer(j), sub), wide_send.at[2], wide_recv.at[2])
-    landed(line, n_y - 1, near_recv.at[1])
+    for i in range(2, 6):
+        landed(line, 1, hop_recv.at[i])
+    for i in range(6, 8):
+        landed(line.at[0], 1, hop_recv.at[i])
 
     def place_of(code):
         rest = lax.rem(code, group)
@@ -319,12 +336,10 @@
     loads[3].wait()
     for s in range(SLOTS):
         from_recycled = jnp.sum(recycled[:, s, :] * update[0:K], axis=0, keepdims=True) * masks[s]
-        solution_ref[s : s + 1, :] = from_recycled + sum(
-            least[j] * basis[j][s] for j in range(STEPS)
-        )
-        residual_ref[s : s + 1, :] = residuals[s] - sum(
-            weights[i] * basis[i][s] for i in range(STEPS + 1)
-        )
+        parts_ref[0, s : s + 1, :] = from_recycled
+        parts_ref[1, s : s + 1, :] = sum(least[j] * basis[j][s] for j in range(STEPS))
+        parts_ref[2, s : s + 1, :] = residuals[s]
+        parts_ref[3, s : s + 1, :] = sum(weights[i] * basis[i][s] for i in range(STEPS + 1))
 
     landed(sub_wide, n_sub - 1, wide_send.at[0])
     landed(z_wide, n_z - 1, wide_send.at[1])
@@ -349,14 +364,13 @@
         anywhere = pl.BlockSpec(memory_space=pl.ANY)
         scalars = pl.BlockSpec(memory_space=pltpu.SMEM)
         vectors = pl.BlockSpec(memory_space=pltpu.VMEM)
-        shape = jax.ShapeDtypeStruct(load_vector.shape, f32)
         dma = pltpu.SemaphoreType.DMA
         asks = (3 * CORES, 1, LANES)
-        return pl.pallas_call(
+        parts = pl.pallas_call(
             functools.partial(kernel, n_dom, n_z, n_sub),
-            out_shape=(shape, shape),
+            out_shape=jax.ShapeDtypeStruct((4, *load_vector.shape), f32),
             in_specs=[anywhere] * 4 + [scalars] * 3,
-            out_specs=(vectors, vectors),
+            out_specs=vectors,
             scratch_shapes=[
                 pltpu.VMEM(load_vector.shape, f32),
                 pltpu.VMEM(recycled.shape, f32),
@@ -383,10 +397,11 @@
                 dma((3,)), dma((3,)),
                 dma((STEPS, 3)), dma((STEPS, 3)),
                 dma((STEPS - 1,)), dma((STEPS - 1,)),
-                dma((3,)), dma((3,)),
+                dma((3,)), dma((3,)), dma((8,)),
             ],
             compiler_params=pltpu.CompilerParams(collective_id=0, has_side_effects=True),
         )(load_vector, recycled, images, matrix_tiles, tile_columns, ghost_list, live_counts)
+        return parts[0] + parts[1], parts[2] - parts[3]
 
     both = ("dom", "sub")
     in_specs = (

time: 90.3 us -> 87.2 us (0.966)
  Pallas kernels: 86.6 us -> 84.5 us
  local copies, waits for them, and re-layouts: 1.85 us -> 0 us
  other arithmetic: 0 us -> 1.25 us
    pallas_call x1, Pallas kernels: 86.6 us -> 84.5 us  [local(): pl.pallas_call(functools.partial(kernel, n_dom, n_z, n_sub), out_shape=ja...]
    unnamed x6 -> x0, local copies, waits for them, and re-layouts: 1.85 us -> none
    sub x0 -> x1, other arithmetic: none -> 1.25 us  [local(): return (parts[0] + parts[1], parts[2] - parts[3])]
where the time goes in v3:
time: 87.2 us; the launch traced here: 87 us
  Pallas kernels  84.5 us (97%)
  between operations  1.29 us (1%)
  other arithmetic  1.25 us (1%)
    pallas_call x1, Pallas kernels, local(): pl.pallas_call(functools.partial(kernel, n_dom, n_z, n_sub), out_shape=ja...  84.5 us

profile of v3, /device:TPU:1, one launch (start us, length us, event | category | flops | bytes accessed | tf_op | source)
XLA Modules:
  0.0 87.0 jit_solution(360527592781041230)
XLA Ops:
  1.3 84.5 %shard_map.86 = f32[4,2,128]{2,1,0:T(2,128)} custom-call(f32[2,128]{1,0:T(2,128)} %load_hbm.1, f32[40,2,128]{2,1,0:T(2,128)} %recycled_hbm.1, f32[40,2,128]{2,1,0:T(2,128)} %images_hbm.1, f32[2,8,128,128]{3,2,1,0:T(8,128)} %tiles_hbm.1, s32[2,8]{1,0:T(2,128)} %columns_ref.1, s32[1,4]{1,0:T(1,128)} %ghosts_ref.1, s32[1]{0:T(128)S(6)} %copy.9.live_ref), custom_call_target="tpu_custom_call" | custom-call | tf_op jit(solution)/shard_map/pallas_call | solution.py:369
  85.7 1.3 %subtract_bitcast_fusion = (f32[2,128]{1,0:T(2,128)}, f32[2,128]{1,0:T(2,128)}) fusion(f32[4,2,128]{2,1,0:T(2,128)} %shard_map.86), kind=kLoop, calls=%fused_computation | loop fusion | flops 512 | bytes 6144 | tf_op jit(solution)/shard_map/sub | solution.py:404

commit v4 on v3

--- a/solution.py
+++ b/solution.py
@@ -61,7 +61,7 @@
 ):
     halos, more = more[: STEPS - 1], more[STEPS - 1 :]
     line, asks, ask, asked, answers, answered, *more = more
-    sub_wide, x_wide, z_wide, sub_thin, x_thin, z_thin, load_sem, *more = more
+    sub_wide, x_wide, z_wide, sub_thin, plane_thin, load_sem, *more = more
     wide_send, wide_recv, thin_send, thin_recv, halo_send, halo_recv, near_send, near_recv, hop_recv = more
     n_x = n_dom // n_z
     n_y = n_sub // CORES
@@ -89,6 +89,10 @@
     def z_peer(step):
         return x * n_z + lax.rem(z + far_first(step, n_z), n_z)
 
+    def plane_peer(i, j):
+        across = lax.rem(x + far_first(i, n_x), n_x)
+        return across * n_z + lax.rem(z + far_first(j, n_z), n_z)
+
     def each(count, body):
         def wrapped(step, carry):
             body(step)
@@ -96,6 +100,10 @@
 
         lax.fori_loop(0, count, wrapped, 0)
 
+    def each_of_plane(body):
+        each(n_x - 1, lambda i: each(n_z, lambda j: body(plane_peer(i, j))))
+        each(n_z - 1, lambda j: body(plane_peer(n_x - 1, j)))
+
     barrier = pltpu.get_barrier_semaphore()
 
     def greet(device):
@@ -105,8 +113,7 @@
     each(n_sub, lambda j: greet((before, sub_peer(j))))
     each(n_sub, lambda j: greet((after, sub_peer(j))))
     each(n_sub - 1, lambda j: greet((dom, sub_peer(j))))
-    each(n_x - 1, lambda j: greet((x_peer(j), sub)))
-    each(n_z - 1, lambda j: greet((z_peer(j), sub)))
+    each_of_plane(lambda peer: greet((peer, sub)))
 
     masks = [jnp.where(live_ref[0] > s, 1.0, 0.0) for s in range(SLOTS)]
     rows, lanes = iota((ROWS, LANES), 0), iota((ROWS, LANES), 1)
@@ -137,7 +144,7 @@
         )
         packed = packed + (pltpu.roll(block, 41 * part, 1) if part else block)
 
-    pl.semaphore_wait(barrier, 3 * n_sub - 1 + n_x - 1 + n_z - 1)
+    pl.semaphore_wait(barrier, 3 * n_sub - 1 + n_dom - 1)
 
     def push(src, dst, send, recv, device):
         pltpu.make_async_remote_copy(
@@ -276,20 +283,18 @@
         for s in range(SLOTS):
             stack[s, NEW : NEW + 1, :] = image[s]
         grid = sum(stack[s] * image[s] for s in range(SLOTS))
-        across, down, along = sub_thin.at[step], z_thin.at[step], x_thin.at[step]
+        across, plane = sub_thin.at[step], plane_thin.at[step]
         send, recv = thin_send.at[step], thin_recv.at[step]
         across[sub] = jnp.sum(grid.T, axis=0, keepdims=True)
         spread(across, sub, n_sub, lambda j: (dom, sub_peer(j)), send.at[0], recv.at[0])
         if not last:
             send_halo(image, step)
         landed(across, n_sub - 1, recv.at[0])
-        down[z] = jnp.sum(across[...], axis=0)
-        spread(down, z, n_z, lambda j: (z_peer(j), sub), send.at[1], recv.at[1])
-        landed(down, n_z - 1, recv.at[1])
-        along[x] = jnp.sum(down[...], axis=0)
-        spread(along, x, n_x, lambda j: (x_peer(j), sub), send.at[2], recv.at[2])
-        landed(along, n_x - 1, recv.at[2])
-        dots = jnp.sum(along[...], axis=0)
+        plane[dom] = jnp.sum(across[...], axis=0)
+        mine = plane.at[dom]
+        each_of_plane(lambda peer: push(mine, mine, send.at[1], recv.at[1], (peer, sub)))
+        landed(plane, n_dom - 1, recv.at[1])
+        dots = jnp.sum(plane[...], axis=0)
         coef = jnp.sum(inverse * dots, axis=1, keepdims=True)
         product = jnp.sum(unit * dots, axis=1, keepdims=True)
         square = jnp.sum(
@@ -349,8 +354,7 @@
     landed(answers, len(near), near_send.at[2])
     for step in range(STEPS):
         landed(sub_thin.at[step], n_sub - 1, thin_send.at[step, 0])
-        landed(z_thin.at[step], n_z - 1, thin_send.at[step, 1])
-        landed(x_thin.at[step], n_x - 1, thin_send.at[step, 2])
+        landed(plane_thin.at[step], n_dom - 1, thin_send.at[step, 1])
         if step < STEPS - 1:
             landed(halos[step], 3 * group - SLOTS, halo_send.at[step])
 
@@ -391,11 +395,10 @@
                 pltpu.VMEM((n_x, FOLD, LANES), f32),
                 pltpu.VMEM((n_z, FOLD, LANES), f32),
                 pltpu.VMEM((STEPS, n_sub, 1, LANES), f32),
-                pltpu.VMEM((STEPS, n_x, 1, LANES), f32),
-                pltpu.VMEM((STEPS, n_z, 1, LANES), f32),
+                pltpu.VMEM((STEPS, n_dom, 1, LANES), f32),
                 dma((5,)),
                 dma((3,)), dma((3,)),
-                dma((STEPS, 3)), dma((STEPS, 3)),
+                dma((STEPS, 2)), dma((STEPS, 2)),
                 dma((STEPS - 1,)), dma((STEPS - 1,)),
                 dma((3,)), dma((3,)), dma((8,)),
             ],

time: 87.2 us -> 83.4 us (0.956)
  Pallas kernels: 84.5 us -> 80.6 us
    pallas_call x1, Pallas kernels: 84.5 us -> 80.6 us  [local(): pl.pallas_call(functools.partial(kernel, n_dom, n_z, n_sub), out_shape=ja...]
where the time goes in v4:
time: 83.4 us; the launch traced here: 83.2 us
  Pallas kernels  80.6 us (97%)
  between operations  1.29 us (2%)
  other arithmetic  1.25 us (1%)
    pallas_call x1, Pallas kernels, local(): pl.pallas_call(functools.partial(kernel, n_dom, n_z, n_sub), out_shape=ja...  80.6 us

profile of v4, /device:TPU:1, one launch (start us, length us, event | category | flops | bytes accessed | tf_op | source)
XLA Modules:
  0.0 83.2 jit_solution(3900136088575329699)
XLA Ops:
  1.3 80.6 %shard_map.86 = f32[4,2,128]{2,1,0:T(2,128)} custom-call(f32[2,128]{1,0:T(2,128)} %load_hbm.1, f32[40,2,128]{2,1,0:T(2,128)} %recycled_hbm.1, f32[40,2,128]{2,1,0:T(2,128)} %images_hbm.1, f32[2,8,128,128]{3,2,1,0:T(8,128)} %tiles_hbm.1, s32[2,8]{1,0:T(2,128)} %columns_ref.1, s32[1,4]{1,0:T(1,128)} %ghosts_ref.1, s32[1]{0:T(128)S(6)} %copy.9.live_ref), custom_call_target="tpu_custom_call" | custom-call | tf_op jit(solution)/shard_map/pallas_call | solution.py:373
  81.9 1.3 %subtract_bitcast_fusion = (f32[2,128]{1,0:T(2,128)}, f32[2,128]{1,0:T(2,128)}) fusion(f32[4,2,128]{2,1,0:T(2,128)} %shard_map.86), kind=kLoop, calls=%fused_computation | loop fusion | flops 512 | bytes 6144 | tf_op jit(solution)/shard_map/sub | solution.py:407

commit v5 on v4

--- a/solution.py
+++ b/solution.py
@@ -55,9 +55,9 @@
 
 def kernel(
     n_dom, n_z, n_sub,
-    load_hbm, recycled_hbm, images_hbm, tiles_hbm, columns_ref, ghosts_ref, live_ref,
+    load_hbm, recycled_hbm, images_hbm, tiles_hbm, columns_hbm, ghosts_hbm, live_ref,
     parts_ref,
-    source, recycled, images, tiles, stack, ghost_stack, gram, vectors, *more,
+    columns_ref, ghosts_ref, source, recycled, images, tiles, stack, ghost_stack, gram, vectors, *more,
 ):
     halos, more = more[: STEPS - 1], more[STEPS - 1 :]
     line, asks, ask, asked, answers, answered, *more = more
@@ -77,7 +77,11 @@
             [(images_hbm, images), (load_hbm, source), (tiles_hbm, tiles), (recycled_hbm, recycled)]
         )
     ]
-    for load in loads:
+    listings = [
+        pltpu.make_async_copy(ghosts_hbm, ghosts_ref, load_sem.at[5]),
+        pltpu.make_async_copy(columns_hbm, columns_ref, load_sem.at[6]),
+    ]
+    for load in loads + listings:
         load.start()
 
     def sub_peer(step):
@@ -110,11 +114,13 @@
         pl.semaphore_signal(barrier, inc=1, device_id=device, device_id_type=MESH)
 
     before, after = lax.rem(dom + n_dom - 1, n_dom), lax.rem(dom + 1, n_dom)
+    each_of_plane(lambda peer: greet((peer, sub)))
     each(n_sub, lambda j: greet((before, sub_peer(j))))
     each(n_sub, lambda j: greet((after, sub_peer(j))))
     each(n_sub - 1, lambda j: greet((dom, sub_peer(j))))
-    each_of_plane(lambda peer: greet((peer, sub)))
-
+
+    for listing in listings:
+        listing.wait()
     masks = [jnp.where(live_ref[0] > s, 1.0, 0.0) for s in range(SLOTS)]
     rows, lanes = iota((ROWS, LANES), 0), iota((ROWS, LANES), 1)
     row_of = iota((ROWS, 1), 0)
@@ -373,9 +379,11 @@
         parts = pl.pallas_call(
             functools.partial(kernel, n_dom, n_z, n_sub),
             out_shape=jax.ShapeDtypeStruct((4, *load_vector.shape), f32),
-            in_specs=[anywhere] * 4 + [scalars] * 3,
+            in_specs=[anywhere] * 6 + [scalars],
             out_specs=vectors,
             scratch_shapes=[
+                pltpu.SMEM(tile_columns.shape, jnp.int32),
+                pltpu.SMEM(ghost_list.shape, jnp.int32),
                 pltpu.VMEM(load_vector.shape, f32),
                 pltpu.VMEM(recycled.shape, f32),
                 pltpu.VMEM(images.shape, f32),
@@ -396,7 +404,7 @@
                 pltpu.VMEM((n_z, FOLD, LANES), f32),
                 pltpu.VMEM((STEPS, n_sub, 1, LANES), f32),
                 pltpu.VMEM((STEPS, n_dom, 1, LANES), f32),
-                dma((5,)),
+                dma((7,)),
                 dma((3,)), dma((3,)),
                 dma((STEPS, 2)), dma((STEPS, 2)),
                 dma((STEPS - 1,)), dma((STEPS - 1,)),

time: 83.4 us -> 82.8 us (level)
  no operation moved by 1% of the time
where the time goes in v5:
time: 82.8 us; the launch traced here: 82.6 us
  Pallas kernels  80.1 us (97%)
  between operations  1.29 us (2%)
  other arithmetic  1.25 us (2%)
    pallas_call x1, Pallas kernels, local(): pl.pallas_call(functools.partial(kernel, n_dom, n_z, n_sub), out_shape=ja...  80.1 us

profile of v5, /device:TPU:1, one launch (start us, length us, event | category | flops | bytes accessed | tf_op | source)
XLA Modules:
  0.0 82.6 jit_solution(13462319811434210400)
XLA Ops:
  1.3 80.1 %shard_map.86 = f32[4,2,128]{2,1,0:T(2,128)} custom-call(f32[2,128]{1,0:T(2,128)} %load_hbm.1, f32[40,2,128]{2,1,0:T(2,128)} %recycled_hbm.1, f32[40,2,128]{2,1,0:T(2,128)} %images_hbm.1, f32[2,8,128,128]{3,2,1,0:T(8,128)} %tiles_hbm.1, s32[2,8]{1,0:T(2,128)} %columns_hbm.1, s32[1,4]{1,0:T(1,128)} %ghosts_hbm.1, s32[1]{0:T(128)S(6)} %copy.9.live_ref), custom_call_target="tpu_custom_call" | custom-call | tf_op jit(solution)/shard_map/pallas_call | solution.py:379
  81.4 1.3 %subtract_bitcast_fusion = (f32[2,128]{1,0:T(2,128)}, f32[2,128]{1,0:T(2,128)}) fusion(f32[4,2,128]{2,1,0:T(2,128)} %shard_map.86), kind=kLoop, calls=%fused_computation | loop fusion | flops 512 | bytes 6144 | tf_op jit(solution)/shard_map/sub | solution.py:415
